TPU v7x, 32 devices: a whole 2x2x4 slice. The times are simulated.
32 devices in a mesh: req: 2 (over y), blk: 4 (over z), uly: 4 (over x, core).
Axes of the slice: x: 2, y: 2, z: 4, core: 2. Of those that a mesh axis runs over, the one named last changes fastest.
Arguments:
- video_qkv: bfloat16 [3, 2048, 3072], P(None, ('req', 'blk', 'uly')), parts along dimension 1, may hold values from -16 to 16
- text_qkv: bfloat16 [3, 64, 3072], P(None, ('req', 'blk', 'uly')), parts along dimension 1, may hold values from -9.5625 to 9.5625
- video_gate: float32 [6144], P('req'), parts along dimension 0, may hold values from 1 to 4
- text_gate: float32 [6144], P('req'), parts along dimension 0, may hold values from 1 to 4
Outputs:
- video_out: bfloat16 [2048, 3072], P(('req', 'blk', 'uly')), parts along dimension 0
- text_out: bfloat16 [64, 3072], P(('req', 'blk', 'uly')), parts along dimension 0
There are 2 independent parts, one for each index of `req`. A program takes and returns all parts, laid end to end along the dimension named above; each array names one. Nothing has to cross between parts.
All inputs are finite; a program needn't handle non-finite values.
Results may differ from a plain program's by a relative error of at most 0.0085.
Values may be sent and summed in bfloat16 or wider, within the bound.
No kernel may reach another device: no remote copies, remote signals or barrier semaphores. Data moves between devices by JAX's collectives and lax.ppermute only.
A program may use at most 128 MiB of HBM per device.

v0:
```python
import math
import jax
import jax.numpy as jnp
from jax import lax
from jax.sharding import PartitionSpec as P

HEADS = 24
HD = 128


def merge_block(state, queries, block_pair):
    best, total, summed = state
    scale = 1.0 / math.sqrt(queries.shape[-1])
    scores = (
        jnp.einsum("qhd,khd->hqk", queries, block_pair[0], preferred_element_type=jnp.float32)
        * scale
    )
    new_best = jnp.maximum(best, jnp.max(scores, axis=2))
    factor = jnp.exp(best - new_best)
    raised = jnp.exp(scores - new_best[:, :, None])
    total = total * factor + jnp.sum(raised, axis=2)
    product = jnp.einsum(
        "hqk,khd->hqd",
        raised.astype(jnp.bfloat16),
        block_pair[1],
        preferred_element_type=jnp.float32,
    )
    summed = summed * factor[:, :, None] + product
    return (new_best, total, summed)


def attend(video_heads, text_heads):
    heads = video_heads.shape[3]
    width = video_heads.shape[4]
    rows_video = video_heads.shape[1]
    rows_text = text_heads.shape[1]
    joined = jnp.concatenate((video_heads, text_heads), axis=1)
    rows_all = rows_video + rows_text
    joined = joined.reshape(3, rows_all, heads, width)
    queries = joined[0]
    key_pairs = joined[1:]
    initial = (
        jnp.full((heads, rows_all), -jnp.inf, jnp.float32),
        jnp.zeros((heads, rows_all), jnp.float32),
        jnp.zeros((heads, rows_all, width), jnp.float32),
    )
    piece = lax.all_gather(key_pairs, "blk", axis=1, tiled=True)
    count = piece.shape[1] // rows_all

    def one_block(index, inner):
        block_pair = lax.dynamic_slice_in_dim(piece, index * rows_all, rows_all, 1)
        return merge_block(inner, queries, block_pair)

    best, total, summed = lax.fori_loop(0, count, one_block, initial)
    attended = (summed / total[:, :, None]).transpose(1, 0, 2).astype(jnp.bfloat16)
    video_att = attended[:rows_video].reshape(rows_video, 1, heads, width)
    text_att = attended[rows_video:].reshape(rows_text, 1, heads, width)
    return (video_att, text_att)


def on_device(video_qkv, text_qkv, video_gate, text_gate):
    groups = lax.axis_size("uly")
    local_heads = HEADS // groups
    video_rows = video_qkv.shape[1]
    text_rows = text_qkv.shape[1]
    video_split = video_qkv.reshape(3, video_rows, groups, local_heads, HD)
    text_split = text_qkv.reshape(3, text_rows, groups, local_heads, HD)
    video_heads, text_heads = (
        lax.all_to_all(video_split, "uly", split_axis=2, concat_axis=1, tiled=True),
        lax.all_to_all(text_split, "uly", split_axis=2, concat_axis=1, tiled=True),
    )
    video_att, text_att = attend(video_heads, text_heads)
    video_back, text_back = (
        lax.all_to_all(video_att, "uly", split_axis=0, concat_axis=1, tiled=True),
        lax.all_to_all(text_att, "uly", split_axis=0, concat_axis=1, tiled=True),
    )
    video_flat = video_back.reshape(video_rows, HEADS * HD).astype(jnp.float32)
    text_flat = text_back.reshape(text_rows, HEADS * HD).astype(jnp.float32)
    video_out = (video_flat * video_gate[None, :]).astype(jnp.bfloat16)
    text_out = (text_flat * text_gate[None, :]).astype(jnp.bfloat16)
    return (video_out, text_out)


def solution(mesh):
    in_specs = (
        P(None, ("req", "blk", "uly"), None),
        P(None, ("req", "blk", "uly"), None),
        P("req"),
        P("req"),
    )
    out_specs = (P(("req", "blk", "uly"), None), P(("req", "blk", "uly"), None))
    return jax.shard_map(
        on_device, mesh=mesh, in_specs=in_specs, out_specs=out_specs, check_vma=False
    )
```

profile of v0, /device:TPU:0, one launch (start us, length us, event | category | flops | bytes accessed | tf_op | source)
XLA Modules:
  0.0 148.8 jit_solution(10764639887761051975)
XLA Ops:
  7.2 0.8 reshape.38
  8.0 0.6 copy.22
  8.6 4.2 %all-to-all-start.1 = ((bf16[3,2,4,6,128]{4,1,3,0,2:T(2,128)(2,1)}), bf16[3,2,4,6,128]{4,1,3,0,2:T(2,128)(2,1)S(1)}, u32[]{:S(2)}, u32[]{:S(2)}) async-start(bf16[3,2,4,6,128]{4,1,3,0,2:T(2,128)(2,1)} %copy.22), calls=%async_computation.1 | async-start | bytes 73728 | tf_op jit(solution)/shard_map/all_to_all | solution.py:70
  12.9 2.8 %reshape.37 = bf16[3,64,4,6,128]{4,3,2,1,0:T(8,128)(2,1)S(1)} reshape(bf16[3,64,3072]{2,1,0:T(8,128)(2,1)} %param.6) | data formatting | bytes 2359296 | tf_op jit(solution)/shard_map/reshape | solution.py:66
  15.7 1.5 copy.20
  17.2 0.0 all-to-all-done.1
  17.2 3.5 %all-to-all-start = ((bf16[3,64,4,6,128]{4,1,3,0,2:T(8,128)(2,1)}), bf16[3,64,4,6,128]{4,1,3,0,2:T(8,128)(2,1)S(1)}, u32[]{:S(2)}, u32[]{:S(2)}) async-start(bf16[3,64,4,6,128]{4,1,3,0,2:T(8,128)(2,1)} %copy.20), calls=%async_computation | async-start | bytes 2359296 | tf_op jit(solution)/shard_map/all_to_all | solution.py:69
  20.7 0.0 all-gather.3.cloned.1.call-start
  20.8 15.7 %all-to-all-done = bf16[3,64,4,6,128]{4,1,3,0,2:T(8,128)(2,1)S(1)} async-done(((bf16[3,64,4,6,128]{4,1,3,0,2:T(8,128)(2,1)}), bf16[3,64,4,6,128]{4,1,3,0,2:T(8,128)(2,1)S(1)}, u32[]{:S(2)}, u32[]{:S(2)}) %all-to-all-start) | async-done | bytes 1179680 | tf_op jit(solution)/shard_map/all_to_all | solution.py:69
  36.5 0.1 copy.21
  36.6 1.0 fusion.12
  37.6 0.0 all-gather.3.cloned.1.call-update
  37.7 66.0 %all-gather.3.cloned.1.call-done = bf16[2,1056,1,6,128]{4,1,3,0,2:T(8,128)(2,1)} async-done(((bf16[2,264,1,6,128]{4,1,3,0,2:T(8,128)(2,1)}), bf16[2,1056,1,6,128]{4,1,3,0,2:T(8,128)(2,1)}) %all-gather.3.cloned.1.call-update) | async-done | bytes 3244048 | tf_op jit(solution)/shard_map/all_gather | solution.py:47
  103.7 16.6 %while.18 = (s32[]{:T(128)}, f32[6,264]{1,0:T(8,128)S(1)}, f32[6,264]{1,0:T(8,128)S(1)}, f32[6,264,128]{2,1,0:T(8,128)S(1)}, bf16[2,1056,6,128]{3,1,2,0:T(8,128)...) while((s32[]{:T(128)}, f32[6,264]{1,0:T(8,128)S(1)}, ...), condition=%wide.region_3.0_spmd.clone, body=%wide.region_0.0_spmd.clone.sunk | while | flops 218067712 | bytes 7958215 | solution.py:54
  103.7 1.6 %bitcast_reduce_fusion.2 = (f32[6,264]{1,0:T(8,128)S(1)}, f32[6,264,264]{2,1,0:T(8,128)S(1)}) fusion(bf16[264,6,128]{2,0,1:T(8,128)(2,1)S(1)} %get-tuple-element.223, bf16[2,1056,6,128]{3,1,2,0:T(8,128)(2,1)} %get-tuple-element.222, s32[]{:T(128)S(6)} %select_n.9), kind=kOutput, calls=%fused_computation.1.clone.1 | convolution fusion | flops 107887824 | bytes 2490052 | tf_op jit(solution)/shard_map/while/body/eval_jaxpr/qhd,khd->hqk/dot_general | solution.py:15
  105.3 0.4 fusion.24
  105.8 2.0 %convolution_add_fusion.2 = f32[6,264,128]{2,1,0:T(8,128)S(1)} fusion(f32[6,264,264]{2,1,0:T(8,128)S(1)} %get-tuple-element.193, f32[6,264]{1,0:T(8,128)S(1)} %select_maximum_fusion.2, f32[6,264,128]{2,1,0:T(8,128)S(1)} %get-tuple-element.210, bf16[2,1056,6,128]{3,1,2,0:T(8,128)(2,1)} %get-tuple-element.222, s32[]{:T(128)S(6)} %add.53, ...), kind=kOutput, calls=%fused_computation.5.clone.1 | convolution fusion | flops 108915840 | bytes 3712905 | tf_op jit(solution)/shard_map/while/body/eval_jaxpr/hqk,khd->hqd/dot_general | solution.py:22
  107.8 1.6 %bitcast_reduce_fusion.2 = (f32[6,264]{1,0:T(8,128)S(1)}, f32[6,264,264]{2,1,0:T(8,128)S(1)}) fusion(bf16[264,6,128]{2,0,1:T(8,128)(2,1)S(1)} %get-tuple-element.223, bf16[2,1056,6,128]{3,1,2,0:T(8,128)(2,1)} %get-tuple-element.222, s32[]{:T(128)S(6)} %select_n.9), kind=kOutput, calls=%fused_computation.1.clone.1 | convolution fusion | flops 107887824 | bytes 2490052 | tf_op jit(solution)/shard_map/while/body/eval_jaxpr/qhd,khd->hqk/dot_general | solution.py:15
  109.5 0.4 fusion.24
  109.9 2.0 %convolution_add_fusion.2 = f32[6,264,128]{2,1,0:T(8,128)S(1)} fusion(f32[6,264,264]{2,1,0:T(8,128)S(1)} %get-tuple-element.193, f32[6,264]{1,0:T(8,128)S(1)} %select_maximum_fusion.2, f32[6,264,128]{2,1,0:T(8,128)S(1)} %get-tuple-element.210, bf16[2,1056,6,128]{3,1,2,0:T(8,128)(2,1)} %get-tuple-element.222, s32[]{:T(128)S(6)} %add.53, ...), kind=kOutput, calls=%fused_computation.5.clone.1 | convolution fusion | flops 108915840 | bytes 3712905 | tf_op jit(solution)/shard_map/while/body/eval_jaxpr/hqk,khd->hqd/dot_general | solution.py:22
  112.0 1.6 %bitcast_reduce_fusion.2 = (f32[6,264]{1,0:T(8,128)S(1)}, f32[6,264,264]{2,1,0:T(8,128)S(1)}) fusion(bf16[264,6,128]{2,0,1:T(8,128)(2,1)S(1)} %get-tuple-element.223, bf16[2,1056,6,128]{3,1,2,0:T(8,128)(2,1)} %get-tuple-element.222, s32[]{:T(128)S(6)} %select_n.9), kind=kOutput, calls=%fused_computation.1.clone.1 | convolution fusion | flops 107887824 | bytes 2490052 | tf_op jit(solution)/shard_map/while/body/eval_jaxpr/qhd,khd->hqk/dot_general | solution.py:15
  113.6 0.4 fusion.24
  114.1 2.0 %convolution_add_fusion.2 = f32[6,264,128]{2,1,0:T(8,128)S(1)} fusion(f32[6,264,264]{2,1,0:T(8,128)S(1)} %get-tuple-element.193, f32[6,264]{1,0:T(8,128)S(1)} %select_maximum_fusion.2, f32[6,264,128]{2,1,0:T(8,128)S(1)} %get-tuple-element.210, bf16[2,1056,6,128]{3,1,2,0:T(8,128)(2,1)} %get-tuple-element.222, s32[]{:T(128)S(6)} %add.53, ...), kind=kOutput, calls=%fused_computation.5.clone.1 | convolution fusion | flops 108915840 | bytes 3712905 | tf_op jit(solution)/shard_map/while/body/eval_jaxpr/hqk,khd->hqd/dot_general | solution.py:22
  116.2 1.6 %bitcast_reduce_fusion.2 = (f32[6,264]{1,0:T(8,128)S(1)}, f32[6,264,264]{2,1,0:T(8,128)S(1)}) fusion(bf16[264,6,128]{2,0,1:T(8,128)(2,1)S(1)} %get-tuple-element.223, bf16[2,1056,6,128]{3,1,2,0:T(8,128)(2,1)} %get-tuple-element.222, s32[]{:T(128)S(6)} %select_n.9), kind=kOutput, calls=%fused_computation.1.clone.1 | convolution fusion | flops 107887824 | bytes 2490052 | tf_op jit(solution)/shard_map/while/body/eval_jaxpr/qhd,khd->hqk/dot_general | solution.py:15
  117.8 0.4 fusion.24
  118.3 2.0 %convolution_add_fusion.2 = f32[6,264,128]{2,1,0:T(8,128)S(1)} fusion(f32[6,264,264]{2,1,0:T(8,128)S(1)} %get-tuple-element.193, f32[6,264]{1,0:T(8,128)S(1)} %select_maximum_fusion.2, f32[6,264,128]{2,1,0:T(8,128)S(1)} %get-tuple-element.210, bf16[2,1056,6,128]{3,1,2,0:T(8,128)(2,1)} %get-tuple-element.222, s32[]{:T(128)S(6)} %add.53, ...), kind=kOutput, calls=%fused_computation.5.clone.1 | convolution fusion | flops 108915840 | bytes 3712905 | tf_op jit(solution)/shard_map/while/body/eval_jaxpr/hqk,khd->hqd/dot_general | solution.py:22
  120.3 0.0 copy-start.1
  120.3 0.1 copy.24
  120.5 0.4 fusion.13
  120.8 0.6 slice_bitcast_fusion.1
  121.4 3.3 %all-to-all-start.3 = ((bf16[8,1,6,128]{3,2,1,0:T(8,128)(2,1)}), bf16[8,1,6,128]{3,2,1,0:T(8,128)(2,1)S(1)}, u32[]{:S(2)}, u32[]{:S(2)}) async-start(bf16[8,1,6,128]{3,2,1,0:T(8,128)(2,1)} %slice_bitcast_fusion.1), calls=%async_computation.3 | async-start | bytes 32768 | tf_op jit(solution)/shard_map/all_to_all | solution.py:75
  124.7 0.8 slice_bitcast_fusion
  125.5 0.0 copy-start
  125.5 3.0 %all-to-all-done.3 = bf16[8,1,6,128]{3,2,1,0:T(8,128)(2,1)S(1)} async-done(((bf16[8,1,6,128]{3,2,1,0:T(8,128)(2,1)}), bf16[8,1,6,128]{3,2,1,0:T(8,128)(2,1)S(1)}, u32[]{:S(2)}, u32[]{:S(2)}) %all-to-all-start.3) | async-done | bytes 12320 | tf_op jit(solution)/shard_map/all_to_all | solution.py:75
  128.5 3.5 %all-to-all-start.2 = ((bf16[256,1,6,128]{3,2,1,0:T(8,128)(2,1)}), bf16[256,1,6,128]{3,2,1,0:T(8,128)(2,1)S(1)}, u32[]{:S(2)}, u32[]{:S(2)}) async-start(bf16[256,1,6,128]{3,2,1,0:T(8,128)(2,1)} %slice_bitcast_fusion), calls=%async_computation.2 | async-start | bytes 1048576 | tf_op jit(solution)/shard_map/all_to_all | solution.py:74
  132.0 0.0 copy-done.1
  132.0 0.6 multiply_convert_fusion.1
  132.7 8.1 %all-to-all-done.2 = bf16[256,1,6,128]{3,2,1,0:T(8,128)(2,1)S(1)} async-done(((bf16[256,1,6,128]{3,2,1,0:T(8,128)(2,1)}), bf16[256,1,6,128]{3,2,1,0:T(8,128)(2,1)S(1)}, u32[]{:S(2)}, u32[]{:S(2)}) %all-to-all-start.2) | async-done | bytes 393248 | tf_op jit(solution)/shard_map/all_to_all | solution.py:74
  140.8 0.1 copy_bitcast_fusion
  140.9 0.2 reshape.41
  141.1 0.0 copy-done
  141.1 0.8 multiply_convert_fusion
  (19 shorter events, 0.2 us)
Async XLA Ops:
  8.6 8.6 %all-to-all-start.1 = ((bf16[3,2,4,6,128]{4,1,3,0,2:T(2,128)(2,1)}), bf16[3,2,4,6,128]{4,1,3,0,2:T(2,128)(2,1)S(1)}, u32[]{:S(2)}, u32[]{:S(2)}) async-start(bf16[3,2,4,6,128]{4,1,3,0,2:T(2,128)(2,1)} %copy.22), calls=%async_computation.1 | async-start | bytes 73728 | tf_op jit(solution)/shard_map/all_to_all | solution.py:70
  17.2 19.3 %all-to-all-start = ((bf16[3,64,4,6,128]{4,1,3,0,2:T(8,128)(2,1)}), bf16[3,64,4,6,128]{4,1,3,0,2:T(8,128)(2,1)S(1)}, u32[]{:S(2)}, u32[]{:S(2)}) async-start(bf16[3,64,4,6,128]{4,1,3,0,2:T(8,128)(2,1)} %copy.20), calls=%async_computation | async-start | bytes 2359296 | tf_op jit(solution)/shard_map/all_to_all | solution.py:69
  20.7 83.0 %all-gather.3.cloned.1.call-start = ((), (), s32[]{:S(2)}) async-start(), calls=%async_computation.4 | async-start | bytes 4055040 | tf_op jit(solution)/shard_map/all_gather | solution.py:47
  120.3 11.7 %copy-start.1 = (f32[3072]{0:T(1024)S(1)}, f32[3072]{0:T(1024)}, u32[]{:S(2)}) copy-start(f32[3072]{0:T(1024)} %param.9) | copy-start | bytes 36868
  121.4 7.1 %all-to-all-start.3 = ((bf16[8,1,6,128]{3,2,1,0:T(8,128)(2,1)}), bf16[8,1,6,128]{3,2,1,0:T(8,128)(2,1)S(1)}, u32[]{:S(2)}, u32[]{:S(2)}) async-start(bf16[8,1,6,128]{3,2,1,0:T(8,128)(2,1)} %slice_bitcast_fusion.1), calls=%async_computation.3 | async-start | bytes 32768 | tf_op jit(solution)/shard_map/all_to_all | solution.py:75
  125.5 15.6 %copy-start = (f32[3072]{0:T(1024)S(1)}, f32[3072]{0:T(1024)}, u32[]{:S(2)}) copy-start(f32[3072]{0:T(1024)} %param.8) | copy-start | bytes 36868
  128.5 12.3 %all-to-all-start.2 = ((bf16[256,1,6,128]{3,2,1,0:T(8,128)(2,1)}), bf16[256,1,6,128]{3,2,1,0:T(8,128)(2,1)S(1)}, u32[]{:S(2)}, u32[]{:S(2)}) async-start(bf16[256,1,6,128]{3,2,1,0:T(8,128)(2,1)} %slice_bitcast_fusion), calls=%async_computation.2 | async-start | bytes 1048576 | tf_op jit(solution)/shard_map/all_to_all | solution.py:74
Sparse Core Ops, SparseCore 0:
  37.7 65.8 all-gather.2
where the time goes:
time: 150 us; the launch traced here: 149 us
  waiting for transfers between devices  92.8 us (62%)
  starting transfers between devices  14.5 us (10%)
  matrix products  14.5 us (10%)
  between operations  14.2 us (9%)
  local copies, waits for them, and re-layouts  7.71 us (5%)
  other arithmetic  4.76 us (3%)
    all_gather x1, waiting for transfers between devices, attend(): piece = lax.all_gather(key_pairs, 'blk', axis=1, tiled=True)  66 us
    all_to_all x1, waiting for transfers between devices, on_device(): lax.all_to_all(video_split, 'uly', split_axis=2, concat_axis=1, tiled=True)  15.7 us
    all_to_all x1, waiting for transfers between devices, on_device(): lax.all_to_all(video_att, 'uly', split_axis=0, concat_axis=1, tiled=True)  8.12 us
    dot_general x4, matrix products, merge_block(): jnp.einsum('hqk,khd->hqd', raised.astype(jnp.bfloat16), block_pair[1], pr...  8.08 us
    dot_general x4, matrix products, merge_block(): jnp.einsum('qhd,khd->hqk', queries, block_pair[0], preferred_element_type...  6.46 us
    reshape x2, local copies, waits for them, and re-layouts, on_device(): video_split = video_qkv.reshape(3, video_rows, groups, local_heads, HD)  4.32 us
    all_to_all x1, starting transfers between devices, on_device(): lax.all_to_all(text_split, 'uly', split_axis=2, concat_axis=1, tiled=True)  4.24 us
    all_to_all x1, starting transfers between devices, on_device(): lax.all_to_all(video_split, 'uly', split_axis=2, concat_axis=1, tiled=True)  3.53 us
  transfers between devices with their start and end apart: 5, of which 4 were waited for; matrix products, arithmetic and copies ran while one was open for 4% of the time, Pallas kernels for 0%

commit v1 on v0

--- a/solution.py
+++ b/solution.py
@@ -44,7 +44,17 @@
         jnp.zeros((heads, rows_all), jnp.float32),
         jnp.zeros((heads, rows_all, width), jnp.float32),
     )
-    piece = lax.all_gather(key_pairs, "blk", axis=1, tiled=True)
+    size, here, width_2 = (lax.axis_size("blk"), lax.axis_index("blk"), key_pairs.shape[1])
+    right = [(i, (i + 1) % size) for i in range(size)]
+    piece = jnp.zeros(
+        (*key_pairs.shape[:1], size * width_2, *key_pairs.shape[1 + 1 :]), key_pairs.dtype
+    )
+    block = key_pairs
+    for step in range(size):
+        holder = (here - step) % size
+        piece = lax.dynamic_update_slice_in_dim(piece, block, holder * width_2, axis=1)
+        if step < size - 1:
+            block = lax.ppermute(block, "blk", right)
     count = piece.shape[1] // rows_all
 
     def one_block(index, inner):

time: 150 us -> 138 us (0.920)
  between operations: 14.2 us -> 0.79 us
  waiting for transfers between devices: 92.8 us -> 83.6 us
  local copies, waits for them, and re-layouts: 7.71 us -> 15.2 us
  starting transfers between devices: 14.5 us -> 16.6 us
    all_gather x1 -> x0, waiting for transfers between devices: 66 us -> none  [attend(): piece = lax.all_gather(key_pairs, 'blk', axis=1, tiled=True)]
    ppermute x0 -> x3, waiting for transfers between devices: none -> 56.8 us  [attend(): block = lax.ppermute(block, 'blk', right)]
    dynamic_update_slice x0 -> x3, local copies, waits for them, and re-layouts: none -> 5.43 us  [attend(): lax.dynamic_update_slice_in_dim(piece, block, holder * width_2, axis=1)]
    ppermute x0 -> x3, starting transfers between devices: none -> 2.12 us  [attend(): block = lax.ppermute(block, 'blk', right)]
    broadcast_in_dim x0 -> x1, local copies, waits for them, and re-layouts: none -> 2.1 us  [attend(): jnp.zeros((*key_pairs.shape[:1], size * width_2, *key_pairs.shape[1 + 1:]...]
  transfers between devices with their start and end apart: 5 -> 7, of which waited for: 4 -> 6; matrix products, arithmetic and copies ran while one was open for 4% -> 7% of each run, Pallas kernels for 0% -> 0%
where the time goes in v1:
time: 138 us; the launch traced here: 137 us
  waiting for transfers between devices  83.6 us (61%)
  starting transfers between devices  16.6 us (12%)
  local copies, waits for them, and re-layouts  15.2 us (11%)
  matrix products  15 us (11%)
  other arithmetic  5.67 us (4%)
    ppermute x3, waiting for transfers between devices, attend(): block = lax.ppermute(block, 'blk', right)  56.8 us
    all_to_all x1, waiting for transfers between devices, on_device(): lax.all_to_all(video_split, 'uly', split_axis=2, concat_axis=1, tiled=True)  15.7 us
    all_to_all x1, waiting for transfers between devices, on_device(): lax.all_to_all(video_att, 'uly', split_axis=0, concat_axis=1, tiled=True)  8.12 us
    dot_general x4, matrix products, merge_block(): jnp.einsum('hqk,khd->hqd', raised.astype(jnp.bfloat16), block_pair[1], pr...  8.08 us
    dot_general x4, matrix products, merge_block(): jnp.einsum('qhd,khd->hqk', queries, block_pair[0], preferred_element_type...  6.91 us
    dynamic_update_slice x3, local copies, waits for them, and re-layouts, attend(): lax.dynamic_update_slice_in_dim(piece, block, holder * width_2, axis=1)  5.43 us
    reshape x2, local copies, waits for them, and re-layouts, on_device(): video_split = video_qkv.reshape(3, video_rows, groups, local_heads, HD)  4.32 us
    all_to_all x1, starting transfers between devices, on_device(): lax.all_to_all(text_split, 'uly', split_axis=2, concat_axis=1, tiled=True)  4.24 us
  transfers between devices with their start and end apart: 7, of which 6 were waited for; matrix products, arithmetic and copies ran while one was open for 7% of the time, Pallas kernels for 0%

profile of v1, /device:TPU:0, one launch (start us, length us, event | category | flops | bytes accessed | tf_op | source)
XLA Modules:
  0.0 137.1 jit_solution(18054635838747636413)
XLA Ops:
  0.6 0.8 reshape.38
  1.4 0.6 copy.22
  2.1 4.2 %all-to-all-start.1 = ((bf16[3,2,4,6,128]{4,1,3,0,2:T(2,128)(2,1)}), bf16[3,2,4,6,128]{4,1,3,0,2:T(2,128)(2,1)S(1)}, u32[]{:S(2)}, u32[]{:S(2)}) async-start(bf16[3,2,4,6,128]{4,1,3,0,2:T(2,128)(2,1)} %copy.22), calls=%async_computation.1 | async-start | bytes 73728 | tf_op jit(solution)/shard_map/all_to_all | solution.py:80
  6.3 2.8 %reshape.37 = bf16[3,64,4,6,128]{4,3,2,1,0:T(8,128)(2,1)S(1)} reshape(bf16[3,64,3072]{2,1,0:T(8,128)(2,1)} %param.6) | data formatting | bytes 2359296 | tf_op jit(solution)/shard_map/reshape | solution.py:76
  9.2 1.5 %copy.20 = bf16[3,64,4,6,128]{4,1,3,0,2:T(8,128)(2,1)} copy(bf16[3,64,4,6,128]{4,3,2,1,0:T(8,128)(2,1)S(1)} %reshape.37) | data formatting | bytes 2359296 | tf_op jit(solution)/shard_map/reshape | solution.py:76
  10.6 0.0 all-to-all-done.1
  10.6 3.5 %all-to-all-start = ((bf16[3,64,4,6,128]{4,1,3,0,2:T(8,128)(2,1)}), bf16[3,64,4,6,128]{4,1,3,0,2:T(8,128)(2,1)S(1)}, u32[]{:S(2)}, u32[]{:S(2)}) async-start(bf16[3,64,4,6,128]{4,1,3,0,2:T(8,128)(2,1)} %copy.20), calls=%async_computation | async-start | bytes 2359296 | tf_op jit(solution)/shard_map/all_to_all | solution.py:79
  14.2 15.7 %all-to-all-done = bf16[3,64,4,6,128]{4,1,3,0,2:T(8,128)(2,1)S(1)} async-done(((bf16[3,64,4,6,128]{4,1,3,0,2:T(8,128)(2,1)}), bf16[3,64,4,6,128]{4,1,3,0,2:T(8,128)(2,1)S(1)}, u32[]{:S(2)}, u32[]{:S(2)}) %all-to-all-start) | async-done | bytes 1179680 | tf_op jit(solution)/shard_map/all_to_all | solution.py:79
  30.0 0.1 copy.21
  30.1 2.1 %broadcast_in_dim.24 = bf16[2,1056,6,128]{3,1,2,0:T(8,128)(2,1)} broadcast(bf16[]{:T(256)} %constant.87.clone.1), dimensions={} | broadcast | bytes 3244034 | tf_op jit(solution)/shard_map/broadcast_in_dim | solution.py:49
  32.2 1.1 constant_dynamic-update-slice_fusion.3
  33.3 2.1 %collective-permute-start = (bf16[2,264,6,128]{3,1,2,0:T(8,128)(2,1)S(1)}, bf16[2,264,6,128]{3,1,2,0:T(8,128)(2,1)S(1)}, u32[]{:S(2)}, u32[]{:S(2)}) collective-permute-start(bf16[2,264,6,128]{3,1,2,0:T(8,128)(2,1)S(1)} %get-tuple-element.150), channel_id=1, source_target_pairs={{0,4},{4,8},{8,12},{12,0},{1,5},{5,9},{9,13},{13,1},{2,6},{6,10},{... | collective-permute-start | bytes 2433032 | tf_op jit(solution)/shard_map/ppermute | solution.py:57
  35.4 19.8 %collective-permute-done = bf16[2,264,6,128]{3,1,2,0:T(8,128)(2,1)S(1)} collective-permute-done((bf16[2,264,6,128]{3,1,2,0:T(8,128)(2,1)S(1)}, bf16[2,264,6,128]{3,1,2,0:T(8,128)(2,1)S(1)}, u32[]{:S(2)}, u32[]{:S(2)}) %collective-permute-start) | collective-permute-done | bytes 811040 | tf_op jit(solution)/shard_map/ppermute | solution.py:57
  55.2 0.0 collective-permute-start.1
  55.2 20.8 %collective-permute-done.1 = bf16[2,264,6,128]{3,1,2,0:T(8,128)(2,1)} collective-permute-done((bf16[2,264,6,128]{3,1,2,0:T(8,128)(2,1)S(1)}, bf16[2,264,6,128]{3,1,2,0:T(8,128)(2,1)}, u32[]{:S(2)}, u32[]{:S(2)}) %collective-permute-start.1) | collective-permute-done | bytes 811040 | tf_op jit(solution)/shard_map/ppermute | solution.py:57
  76.0 0.0 collective-permute-start.2
  76.0 0.8 fusion.15
  76.8 1.0 constant_dynamic-update-slice_fusion.2
  77.9 2.2 %constant_dynamic-update-slice_fusion.1 = bf16[2,1056,6,128]{3,1,2,0:T(8,128)(2,1)} fusion(bf16[2,1056,6,128]{3,1,2,0:T(8,128)(2,1)} %constant_dynamic-update-slice_fusion.2, bf16[2,264,6,128]{3,1,2,0:T(8,128)(2,1)} %collective-permute-done.1, s32[]{:T(128)S(6)} %select_n.43), kind=kLoop, calls=%fused_computation.35 | loop fusion | bytes 1622020 | tf_op jit(solution)/shard_map/dynamic_update_slice | solution.py:55
  80.1 16.1 %collective-permute-done.2 = bf16[2,264,6,128]{3,1,2,0:T(8,128)(2,1)} collective-permute-done((bf16[2,264,6,128]{3,1,2,0:T(8,128)(2,1)}, bf16[2,264,6,128]{3,1,2,0:T(8,128)(2,1)}, u32[]{:S(2)}, u32[]{:S(2)}) %collective-permute-start.2) | collective-permute-done | bytes 811040 | tf_op jit(solution)/shard_map/ppermute | solution.py:57
  96.2 2.2 %constant_dynamic-update-slice_fusion = bf16[2,1056,6,128]{3,1,2,0:T(8,128)(2,1)} fusion(bf16[2,1056,6,128]{3,1,2,0:T(8,128)(2,1)} %constant_dynamic-update-slice_fusion.1, bf16[2,264,6,128]{3,1,2,0:T(8,128)(2,1)} %collective-permute-done.2, s32[]{:T(128)S(6)} %select_n.45), kind=kLoop, calls=%fused_computation.34 | loop fusion | bytes 1622020 | tf_op jit(solution)/shard_map/dynamic_update_slice | solution.py:55
  98.4 17.1 %while.18 = (s32[]{:T(128)}, f32[6,264]{1,0:T(8,128)S(1)}, f32[6,264]{1,0:T(8,128)S(1)}, f32[6,264,128]{2,1,0:T(8,128)S(1)}, bf16[2,1056,6,128]{3,1,2,0:T(8,128)...) while((s32[]{:T(128)}, f32[6,264]{1,0:T(8,128)S(1)}, ...), condition=%wide.region_3.4_spmd.clone, body=%wide.region_0.3_spmd.clone.sunk | while | flops 218067712 | bytes 7958207 | solution.py:64
  98.4 1.7 %bitcast_reduce_fusion.2 = (f32[6,264]{1,0:T(8,128)S(1)}, f32[6,264,264]{2,1,0:T(8,128)S(1)}) fusion(bf16[264,6,128]{2,0,1:T(8,128)(2,1)} %get-tuple-element.225, bf16[2,1056,6,128]{3,1,2,0:T(8,128)(2,1)} %get-tuple-element.224, s32[]{:T(128)S(6)} %select_n.48), kind=kOutput, calls=%fused_computation.1.clone.1 | convolution fusion | flops 107887824 | bytes 2490052 | tf_op jit(solution)/shard_map/while/body/eval_jaxpr/qhd,khd->hqk/dot_general | solution.py:15
  100.2 0.4 fusion.26
  100.6 2.0 %convolution_add_fusion.2 = f32[6,264,128]{2,1,0:T(8,128)S(1)} fusion(f32[6,264,264]{2,1,0:T(8,128)S(1)} %get-tuple-element.195, f32[6,264]{1,0:T(8,128)S(1)} %select_maximum_fusion.2, f32[6,264,128]{2,1,0:T(8,128)S(1)} %get-tuple-element.212, bf16[2,1056,6,128]{3,1,2,0:T(8,128)(2,1)} %get-tuple-element.224, s32[]{:T(128)S(6)} %add.89, ...), kind=kOutput, calls=%fused_computation.5.clone.1 | convolution fusion | flops 108915840 | bytes 3712905 | tf_op jit(solution)/shard_map/while/body/eval_jaxpr/hqk,khd->hqd/dot_general | solution.py:22
  102.7 1.7 %bitcast_reduce_fusion.2 = (f32[6,264]{1,0:T(8,128)S(1)}, f32[6,264,264]{2,1,0:T(8,128)S(1)}) fusion(bf16[264,6,128]{2,0,1:T(8,128)(2,1)} %get-tuple-element.225, bf16[2,1056,6,128]{3,1,2,0:T(8,128)(2,1)} %get-tuple-element.224, s32[]{:T(128)S(6)} %select_n.48), kind=kOutput, calls=%fused_computation.1.clone.1 | convolution fusion | flops 107887824 | bytes 2490052 | tf_op jit(solution)/shard_map/while/body/eval_jaxpr/qhd,khd->hqk/dot_general | solution.py:15
  104.4 0.4 fusion.26
  104.9 2.0 %convolution_add_fusion.2 = f32[6,264,128]{2,1,0:T(8,128)S(1)} fusion(f32[6,264,264]{2,1,0:T(8,128)S(1)} %get-tuple-element.195, f32[6,264]{1,0:T(8,128)S(1)} %select_maximum_fusion.2, f32[6,264,128]{2,1,0:T(8,128)S(1)} %get-tuple-element.212, bf16[2,1056,6,128]{3,1,2,0:T(8,128)(2,1)} %get-tuple-element.224, s32[]{:T(128)S(6)} %add.89, ...), kind=kOutput, calls=%fused_computation.5.clone.1 | convolution fusion | flops 108915840 | bytes 3712905 | tf_op jit(solution)/shard_map/while/body/eval_jaxpr/hqk,khd->hqd/dot_general | solution.py:22
  107.0 1.7 %bitcast_reduce_fusion.2 = (f32[6,264]{1,0:T(8,128)S(1)}, f32[6,264,264]{2,1,0:T(8,128)S(1)}) fusion(bf16[264,6,128]{2,0,1:T(8,128)(2,1)} %get-tuple-element.225, bf16[2,1056,6,128]{3,1,2,0:T(8,128)(2,1)} %get-tuple-element.224, s32[]{:T(128)S(6)} %select_n.48), kind=kOutput, calls=%fused_computation.1.clone.1 | convolution fusion | flops 107887824 | bytes 2490052 | tf_op jit(solution)/shard_map/while/body/eval_jaxpr/qhd,khd->hqk/dot_general | solution.py:15
  108.7 0.4 fusion.26
  109.2 2.0 %convolution_add_fusion.2 = f32[6,264,128]{2,1,0:T(8,128)S(1)} fusion(f32[6,264,264]{2,1,0:T(8,128)S(1)} %get-tuple-element.195, f32[6,264]{1,0:T(8,128)S(1)} %select_maximum_fusion.2, f32[6,264,128]{2,1,0:T(8,128)S(1)} %get-tuple-element.212, bf16[2,1056,6,128]{3,1,2,0:T(8,128)(2,1)} %get-tuple-element.224, s32[]{:T(128)S(6)} %add.89, ...), kind=kOutput, calls=%fused_computation.5.clone.1 | convolution fusion | flops 108915840 | bytes 3712905 | tf_op jit(solution)/shard_map/while/body/eval_jaxpr/hqk,khd->hqd/dot_general | solution.py:22
  111.2 1.7 %bitcast_reduce_fusion.2 = (f32[6,264]{1,0:T(8,128)S(1)}, f32[6,264,264]{2,1,0:T(8,128)S(1)}) fusion(bf16[264,6,128]{2,0,1:T(8,128)(2,1)} %get-tuple-element.225, bf16[2,1056,6,128]{3,1,2,0:T(8,128)(2,1)} %get-tuple-element.224, s32[]{:T(128)S(6)} %select_n.48), kind=kOutput, calls=%fused_computation.1.clone.1 | convolution fusion | flops 107887824 | bytes 2490052 | tf_op jit(solution)/shard_map/while/body/eval_jaxpr/qhd,khd->hqk/dot_general | solution.py:15
  113.0 0.4 fusion.26
  113.5 2.0 %convolution_add_fusion.2 = f32[6,264,128]{2,1,0:T(8,128)S(1)} fusion(f32[6,264,264]{2,1,0:T(8,128)S(1)} %get-tuple-element.195, f32[6,264]{1,0:T(8,128)S(1)} %select_maximum_fusion.2, f32[6,264,128]{2,1,0:T(8,128)S(1)} %get-tuple-element.212, bf16[2,1056,6,128]{3,1,2,0:T(8,128)(2,1)} %get-tuple-element.224, s32[]{:T(128)S(6)} %add.89, ...), kind=kOutput, calls=%fused_computation.5.clone.1 | convolution fusion | flops 108915840 | bytes 3712905 | tf_op jit(solution)/shard_map/while/body/eval_jaxpr/hqk,khd->hqd/dot_general | solution.py:22
  115.5 0.0 copy-start.1
  115.5 0.1 copy.24
  115.7 0.4 fusion.14
  116.0 0.6 slice_bitcast_fusion.1
  116.6 3.3 %all-to-all-start.3 = ((bf16[8,1,6,128]{3,2,1,0:T(8,128)(2,1)}), bf16[8,1,6,128]{3,2,1,0:T(8,128)(2,1)S(1)}, u32[]{:S(2)}, u32[]{:S(2)}) async-start(bf16[8,1,6,128]{3,2,1,0:T(8,128)(2,1)} %slice_bitcast_fusion.1), calls=%async_computation.3 | async-start | bytes 32768 | tf_op jit(solution)/shard_map/all_to_all | solution.py:85
  119.9 0.8 slice_bitcast_fusion
  120.7 0.0 copy-start
  120.7 3.0 %all-to-all-done.3 = bf16[8,1,6,128]{3,2,1,0:T(8,128)(2,1)S(1)} async-done(((bf16[8,1,6,128]{3,2,1,0:T(8,128)(2,1)}), bf16[8,1,6,128]{3,2,1,0:T(8,128)(2,1)S(1)}, u32[]{:S(2)}, u32[]{:S(2)}) %all-to-all-start.3) | async-done | bytes 12320 | tf_op jit(solution)/shard_map/all_to_all | solution.py:85
  123.7 3.5 %all-to-all-start.2 = ((bf16[256,1,6,128]{3,2,1,0:T(8,128)(2,1)}), bf16[256,1,6,128]{3,2,1,0:T(8,128)(2,1)S(1)}, u32[]{:S(2)}, u32[]{:S(2)}) async-start(bf16[256,1,6,128]{3,2,1,0:T(8,128)(2,1)} %slice_bitcast_fusion), calls=%async_computation.2 | async-start | bytes 1048576 | tf_op jit(solution)/shard_map/all_to_all | solution.py:84
  127.2 0.0 copy-done.1
  127.3 0.6 multiply_convert_fusion.1
  127.9 8.1 %all-to-all-done.2 = bf16[256,1,6,128]{3,2,1,0:T(8,128)(2,1)S(1)} async-done(((bf16[256,1,6,128]{3,2,1,0:T(8,128)(2,1)}), bf16[256,1,6,128]{3,2,1,0:T(8,128)(2,1)S(1)}, u32[]{:S(2)}, u32[]{:S(2)}) %all-to-all-start.2) | async-done | bytes 393248 | tf_op jit(solution)/shard_map/all_to_all | solution.py:84
  136.0 0.1 copy_bitcast_fusion
  136.1 0.2 reshape.41
  136.3 0.0 copy-done
  136.3 0.8 multiply_convert_fusion
  (18 shorter events, 0.2 us)
Async XLA Ops:
  2.1 8.6 %all-to-all-start.1 = ((bf16[3,2,4,6,128]{4,1,3,0,2:T(2,128)(2,1)}), bf16[3,2,4,6,128]{4,1,3,0,2:T(2,128)(2,1)S(1)}, u32[]{:S(2)}, u32[]{:S(2)}) async-start(bf16[3,2,4,6,128]{4,1,3,0,2:T(2,128)(2,1)} %copy.22), calls=%async_computation.1 | async-start | bytes 73728 | tf_op jit(solution)/shard_map/all_to_all | solution.py:80
  10.6 19.3 %all-to-all-start = ((bf16[3,64,4,6,128]{4,1,3,0,2:T(8,128)(2,1)}), bf16[3,64,4,6,128]{4,1,3,0,2:T(8,128)(2,1)S(1)}, u32[]{:S(2)}, u32[]{:S(2)}) async-start(bf16[3,64,4,6,128]{4,1,3,0,2:T(8,128)(2,1)} %copy.20), calls=%async_computation | async-start | bytes 2359296 | tf_op jit(solution)/shard_map/all_to_all | solution.py:79
  33.3 21.9 %collective-permute-start = (bf16[2,264,6,128]{3,1,2,0:T(8,128)(2,1)S(1)}, bf16[2,264,6,128]{3,1,2,0:T(8,128)(2,1)S(1)}, u32[]{:S(2)}, u32[]{:S(2)}) collective-permute-start(bf16[2,264,6,128]{3,1,2,0:T(8,128)(2,1)S(1)} %get-tuple-element.150), channel_id=1, source_target_pairs={{0,4},{4,8},{8,12},{12,0},{1,5},{5,9},{9,13},{13,1},{2,6},{6,10},{... | collective-permute-start | bytes 2433032 | tf_op jit(solution)/shard_map/ppermute | solution.py:57
  55.2 20.8 %collective-permute-start.1 = (bf16[2,264,6,128]{3,1,2,0:T(8,128)(2,1)S(1)}, bf16[2,264,6,128]{3,1,2,0:T(8,128)(2,1)}, u32[]{:S(2)}, u32[]{:S(2)}) collective-permute-start(bf16[2,264,6,128]{3,1,2,0:T(8,128)(2,1)S(1)} %collective-permute-done), channel_id=1, source_target_pairs={{0,4},{4,8},{8,12},{12,0},{1,5},{5,9},{9,13},{13,1},{2,6},{6,10},{... | collective-permute-start | bytes 2433032 | tf_op jit(solution)/shard_map/ppermute | solution.py:57
  76.0 20.2 %collective-permute-start.2 = (bf16[2,264,6,128]{3,1,2,0:T(8,128)(2,1)}, bf16[2,264,6,128]{3,1,2,0:T(8,128)(2,1)}, u32[]{:S(2)}, u32[]{:S(2)}) collective-permute-start(bf16[2,264,6,128]{3,1,2,0:T(8,128)(2,1)} %collective-permute-done.1), channel_id=1, source_target_pairs={{0,4},{4,8},{8,12},{12,0},{1,5},{5,9},{9,13},{13,1},{2,6},{6,10},{... | collective-permute-start | bytes 2433032 | tf_op jit(solution)/shard_map/ppermute | solution.py:57
  115.5 11.7 %copy-start.1 = (f32[3072]{0:T(1024)S(1)}, f32[3072]{0:T(1024)}, u32[]{:S(2)}) copy-start(f32[3072]{0:T(1024)} %param.9) | copy-start | bytes 36868
  116.6 7.1 %all-to-all-start.3 = ((bf16[8,1,6,128]{3,2,1,0:T(8,128)(2,1)}), bf16[8,1,6,128]{3,2,1,0:T(8,128)(2,1)S(1)}, u32[]{:S(2)}, u32[]{:S(2)}) async-start(bf16[8,1,6,128]{3,2,1,0:T(8,128)(2,1)} %slice_bitcast_fusion.1), calls=%async_computation.3 | async-start | bytes 32768 | tf_op jit(solution)/shard_map/all_to_all | solution.py:85
  120.7 15.6 %copy-start = (f32[3072]{0:T(1024)S(1)}, f32[3072]{0:T(1024)}, u32[]{:S(2)}) copy-start(f32[3072]{0:T(1024)} %param.8) | copy-start | bytes 36868
  123.7 12.3 %all-to-all-start.2 = ((bf16[256,1,6,128]{3,2,1,0:T(8,128)(2,1)}), bf16[256,1,6,128]{3,2,1,0:T(8,128)(2,1)S(1)}, u32[]{:S(2)}, u32[]{:S(2)}) async-start(bf16[256,1,6,128]{3,2,1,0:T(8,128)(2,1)} %slice_bitcast_fusion), calls=%async_computation.2 | async-start | bytes 1048576 | tf_op jit(solution)/shard_map/all_to_all | solution.py:84
